TPU v7x, 128 devices: a whole 4x4x4 slice. The times are simulated.
128 devices in a mesh: grp: 2 (over x_lo), dp: 64 (over y, x_hi, z, core).
Axes of the slice: x: 4 (x_hi: 2, x_lo: 2; x = x_hi * 2 + x_lo), y: 4, z: 4, core: 2. Of those that a mesh axis runs over, the one named last changes fastest.
Arguments:
- teacher_in: bfloat16 [32768, 1664], P('dp'), may hold values from -6 to 6
- teacher_gain: float32 [1664], replicated, may hold values from 0.5 to 1.5
- teacher_up: bfloat16 [1664, 4096], P('dp', 'grp'), may hold values from -0.15625 to 0.15625
- teacher_down: bfloat16 [1664, 4096], P('dp', 'grp'), may hold values from -0.09375 to 0.09375
- student_in: bfloat16 [32768, 768], P('dp'), may hold values from -6 to 6
- student_gain: float32 [768], replicated, may hold values from 0.5 to 1.5
- student_up: bfloat16 [768, 1536], P(None, ('grp', 'dp')), may hold values from -0.21875 to 0.21875
- student_down: bfloat16 [1536, 768], P(('grp', 'dp')), may hold values from -0.15625 to 0.15625
- student_head: bfloat16 [768, 1664], P(None, ('grp', 'dp')), may hold values from -0.21875 to 0.21875
- student_proj: bfloat16 [768, 512], P(None, ('grp', 'dp')), may hold values from -1 to 1
- word_table: bfloat16 [49408, 512], P(('grp', 'dp')), may hold values from -6 to 6
- caption_ids: int32 [128, 77], replicated, may hold values from 0 to 49407
- positive: int32 [128], replicated, may hold values from 0 to 127, each once
Outputs:
- loss: float32 [], replicated
- grad_up: float32 [768, 1536], P(None, ('grp', 'dp'))
- grad_down: float32 [1536, 768], P(('grp', 'dp'))
- grad_head: float32 [768, 1664], P(None, ('grp', 'dp'))
- grad_proj: float32 [768, 512], P(None, ('grp', 'dp'))
Inputs may be any that keep to these rules, and one draw needn't show every extreme that they name: Each caption is the positive of exactly one image.
All inputs are finite; a program needn't handle non-finite values.
Results may differ from a plain program's by a relative error of at most 0.0065.
Values may be sent and summed in bfloat16 or wider, within the bound.
A program may use at most 128 MiB of HBM per device.

v0:
```python
import jax
import jax.numpy as jnp
from jax import lax
from jax.sharding import PartitionSpec as P

CAP_LEN = 77
PATCHES = 256
IMG_DEV = 1


def normalize_rows(values, gain):
    center = values - jnp.mean(values, -1, keepdims=True)
    spread = jnp.mean(center * center, -1, keepdims=True)
    return center * lax.rsqrt(spread + 1e-05) * gain


def gelu_tanh(values):
    return jax.nn.gelu(values, approximate=True)


def unit_rows(values):
    return values / jnp.sqrt(jnp.sum(values * values, -1, keepdims=True) + 1e-06)


def local(
    teacher_in,
    teacher_gain,
    teacher_up,
    teacher_down,
    student_in,
    student_gain,
    student_up,
    student_down,
    student_head,
    student_proj,
    word_table,
    caption_ids,
    positive,
):
    contract = (((1,), (1,)), ((), ()))
    grp_index = lax.axis_index("grp")
    dp_index = lax.axis_index("dp")
    n_grp = lax.axis_size("grp")
    n_dp = lax.axis_size("dp")
    devices = n_grp * n_dp
    teacher_width = teacher_in.shape[1]
    rows_teacher = teacher_in.shape[0]
    teacher_normed = normalize_rows(teacher_in.astype(jnp.float32), teacher_gain).astype(
        jnp.bfloat16
    )
    columns = teacher_normed
    hidden = jnp.dot(
        columns,
        lax.all_gather(teacher_up, "dp", axis=0, tiled=True),
        preferred_element_type=jnp.float32,
    )
    teacher_act = gelu_tanh(hidden).astype(jnp.bfloat16)
    partial_value = lax.dot_general(
        teacher_act,
        lax.all_gather(teacher_down, "dp", axis=0, tiled=True),
        contract,
        preferred_element_type=jnp.float32,
    )
    branch = lax.psum_scatter(
        partial_value.astype(jnp.bfloat16), "grp", scatter_dimension=0, tiled=True
    ).astype(jnp.float32)
    own_rows = rows_teacher // n_grp
    target = (
        lax.dynamic_slice_in_dim(teacher_in, grp_index * own_rows, own_rows, 0).astype(jnp.float32)
        + branch
    )
    student_rows = lax.dynamic_slice_in_dim(student_in, grp_index * own_rows, own_rows, 0).astype(
        jnp.float32
    )
    student_width = student_rows.shape[1]
    student_normed = normalize_rows(student_rows, student_gain).astype(jnp.bfloat16)
    gate_out = jnp.dot(
        student_normed,
        lax.all_gather(student_up, ("grp", "dp"), axis=1, tiled=True),
        preferred_element_type=jnp.float32,
    )
    down_whole, head_whole, proj_whole = (
        lax.all_gather(student_down, ("grp", "dp"), axis=0, tiled=True),
        lax.all_gather(student_head, ("grp", "dp"), axis=1, tiled=True),
        lax.all_gather(student_proj, ("grp", "dp"), axis=1, tiled=True),
    )
    student_act = gelu_tanh(gate_out).astype(jnp.bfloat16)
    student_out = student_rows + jnp.dot(
        student_act, down_whole, preferred_element_type=jnp.float32
    )
    student_rounded = student_out.astype(jnp.bfloat16)
    diff = jnp.dot(student_rounded, head_whole, preferred_element_type=jnp.float32) - target
    feature_part = jnp.sum(diff * diff) / teacher_width
    pooled = (jnp.sum(student_out.reshape(IMG_DEV, PATCHES, student_width), 1) / PATCHES).astype(
        jnp.bfloat16
    )
    projected = jnp.dot(pooled, proj_whole, preferred_element_type=jnp.float32)
    proj_norm = jnp.sqrt(jnp.sum(projected * projected, -1, keepdims=True) + 1e-06)
    image_emb = projected / proj_norm
    embed_width = image_emb.shape[1]
    caption_count = caption_ids.shape[0]
    caption_dev = caption_count // devices
    shard_block = grp_index * n_dp + dp_index
    vocab_dev = word_table.shape[0]
    vocab_codes = shard_block * vocab_dev + jnp.arange(vocab_dev, dtype=jnp.int32)
    counts = jnp.sum(
        caption_ids[:, :, None] == vocab_codes[None, None, :], 1, dtype=jnp.float32
    ).astype(jnp.bfloat16)
    partial_words = jnp.dot(counts, word_table, preferred_element_type=jnp.float32) / CAP_LEN
    words = lax.psum(partial_words, ("grp", "dp"))
    caption_all = unit_rows(words)
    caption_own = lax.dynamic_slice_in_dim(caption_all, shard_block * caption_dev, caption_dev, 0)
    gathered = lax.all_gather(image_emb, ("grp", "dp"), axis=0, tiled=True)
    image_all = jnp.transpose(
        gathered.reshape(n_grp, n_dp, IMG_DEV, embed_width), (1, 0, 2, 3)
    ).reshape(-1, embed_width)
    image_first = (dp_index * n_grp + grp_index) * IMG_DEV
    positive_own = lax.dynamic_slice_in_dim(positive, image_first, IMG_DEV, 0)
    scores_own = 100.0 * jnp.dot(image_emb, caption_all.T, precision=lax.Precision.HIGHEST)
    match_own = (
        positive_own[:, None] == jnp.arange(caption_count, dtype=jnp.int32)[None, :]
    ).astype(jnp.float32)
    caption_first = shard_block * caption_dev
    scores_cols = 100.0 * jnp.dot(image_all, caption_own.T, precision=lax.Precision.HIGHEST)
    match_cols = (
        positive[:, None] == (caption_first + jnp.arange(caption_dev, dtype=jnp.int32))[None, :]
    ).astype(jnp.float32)
    contrast_part = jnp.sum(jax.nn.logsumexp(scores_own, 1)) - jnp.sum(match_own * scores_own)
    contrast_part = (
        contrast_part
        + jnp.sum(jax.nn.logsumexp(scores_cols, 0))
        - jnp.sum(match_cols * scores_cols)
    )
    grad_rows = jax.nn.softmax(scores_own, 1) - match_own
    grad_cols = jax.nn.softmax(scores_cols, 0) - match_cols
    grad_far = 100.0 * jnp.dot(grad_cols, caption_own, precision=lax.Precision.HIGHEST)
    grad_far = jnp.transpose(
        grad_far.reshape(n_dp, n_grp, IMG_DEV, embed_width), (1, 0, 2, 3)
    ).reshape(-1, embed_width)
    grad_image = 100.0 * jnp.dot(grad_rows, caption_all, precision=lax.Precision.HIGHEST)
    grad_image = grad_image + lax.psum_scatter(
        grad_far, ("grp", "dp"), scatter_dimension=0, tiled=True
    )
    grad_projected = (
        (grad_image - image_emb * jnp.sum(image_emb * grad_image, -1, keepdims=True)) / proj_norm
    ).astype(jnp.bfloat16)
    proj_part = jnp.dot(pooled.T, grad_projected, preferred_element_type=jnp.float32)
    grad_pooled = lax.dot_general(
        grad_projected, proj_whole, contract, preferred_element_type=jnp.float32
    )
    grad_pred = (2.0 * diff / teacher_width).astype(jnp.bfloat16)
    head_part = jnp.dot(student_rounded.T, grad_pred, preferred_element_type=jnp.float32)
    grad_out = lax.dot_general(grad_pred, head_whole, contract, preferred_element_type=jnp.float32)
    grad_out = (
        (grad_out.reshape(IMG_DEV, PATCHES, student_width) + (grad_pooled / PATCHES)[:, None, :])
        .reshape(-1, student_width)
        .astype(jnp.bfloat16)
    )
    columns = student_act
    grad_down = lax.psum_scatter(
        lax.dot_general(
            columns, grad_out, (((0,), (0,)), ((), ())), preferred_element_type=jnp.float32
        ),
        ("grp", "dp"),
        scatter_dimension=0,
        tiled=True,
    )
    grad_act = lax.dot_general(grad_out, down_whole, contract, preferred_element_type=jnp.float32)
    grad_gate = jax.vjp(gelu_tanh, gate_out)[1](grad_act)[0].astype(jnp.bfloat16)
    up_part = jnp.dot(student_normed.T, grad_gate, preferred_element_type=jnp.float32)
    grad_up, grad_head, grad_proj = (
        lax.psum_scatter(up_part, ("grp", "dp"), scatter_dimension=1, tiled=True),
        lax.psum_scatter(head_part, ("grp", "dp"), scatter_dimension=1, tiled=True),
        lax.psum_scatter(proj_part, ("grp", "dp"), scatter_dimension=1, tiled=True),
    )
    total = lax.psum(feature_part + contrast_part, ("grp", "dp"))
    loss = total / (positive.shape[0] * PATCHES)
    return (loss, grad_up, grad_down, grad_head, grad_proj)


def solution(mesh):
    placed = (
        P("dp", None),
        P(),
        P("dp", "grp"),
        P("dp", "grp"),
        P("dp", None),
        P(),
        P(None, ("grp", "dp")),
        P(("grp", "dp"), None),
        P(None, ("grp", "dp")),
        P(None, ("grp", "dp")),
        P(("grp", "dp"), None),
        P(),
        P(),
    )
    return jax.shard_map(
        local,
        mesh=mesh,
        in_specs=placed,
        out_specs=(
            P(),
            P(None, ("grp", "dp")),
            P(("grp", "dp"), None),
            P(None, ("grp", "dp")),
            P(None, ("grp", "dp")),
        ),
        check_vma=False,
    )
```

profile of v0, /device:TPU:16, one launch (start us, length us, event | category | flops | bytes accessed | tf_op | source)
XLA Modules:
  0.0 1861.4 jit_solution(75165170728293733)
XLA Ops:
  13.5 164.2 %all-gather.6 = bf16[128,4,768]{2,1,0:T(4,128)(2,1)S(1)} all-gather(bf16[1,4,768]{2,1,0:T(4,128)(2,1)} %bitcast.97), channel_id=1, replica_groups=mesh['grp'=2,'dp'=64] {'grp','dp'}, dimensions={0}, use_global_device_ids=true | all-gather | bytes 792576 | tf_op jit(solution)/shard_map/all_gather | solution.py:85
  181.1 172.8 %all-gather.16.cloned.1.call-done = bf16[128,12,768]{2,1,0:T(8,128)(2,1)} async-done(((bf16[1,12,768]{2,1,0:T(8,128)(2,1)}), bf16[128,12,768]{2,1,0:T(8,128)(2,1)}) %all-gather.16.cloned.1.call-update) | async-done | bytes 2359312 | tf_op jit(solution)/shard_map/all_gather | solution.py:83
  353.8 4.9 reshape.194
  358.8 192.1 %all-gather.14.cloned.1.call-done = bf16[128,12,768]{2,1,0:T(8,128)(2,1)} async-done(((bf16[1,12,768]{2,1,0:T(8,128)(2,1)}), bf16[128,12,768]{2,1,0:T(8,128)(2,1)}) %all-gather.14.cloned.1.call-update) | async-done | bytes 2359312 | tf_op jit(solution)/shard_map/all_gather | solution.py:79
  550.9 4.9 reshape.192
  562.9 161.3 %all-gather.7 = f32[128,1,512]{2,1,0:T(1,128)S(1)} all-gather(f32[1,1,512]{2,1,0:T(1,128)S(1)} %bitcast.84), channel_id=2, replica_groups=mesh['grp'=2,'dp'=64] {'grp','dp'}, dimensions={0}, use_global_device_ids=true | all-gather | bytes 264192 | tf_op jit(solution)/shard_map/all_gather | solution.py:113
  740.5 9.1 reshape.200
  749.6 9.1 reshape.198
  758.7 14.6 convolution_convert_fusion
  775.8 114.0 %all-reduce.15.cloned.1.call-done = f32[128,512]{1,0:T(8,128)} async-done(((f32[128,512]{1,0:T(8,128)}), f32[128,512]{1,0:T(8,128)}) %all-reduce.15.cloned.1.call-update) | async-done | bytes 262160
  894.2 191.6 %all-gather.18.cloned.1.call-done = bf16[128,13,768]{2,1,0:T(8,128)(2,1)} async-done(((bf16[1,13,768]{2,1,0:T(8,128)(2,1)}), bf16[128,13,768]{2,1,0:T(8,128)(2,1)}) %all-gather.18.cloned.1.call-update) | async-done | bytes 2555920 | tf_op jit(solution)/shard_map/all_gather | solution.py:84
  1085.8 5.3 reshape.196
  1091.2 26.4 %reduce-scatter.8.cloned.1.call-done = bf16[256,1664]{1,0:T(8,128)(2,1)} async-done(((bf16[512,1664]{1,0:T(8,128)(2,1)}), bf16[256,1664]{1,0:T(8,128)(2,1)}) %reduce-scatter.8.cloned.1.call-update) | async-done | bytes 851984 | tf_op jit(solution)/shard_map/reduce_scatter | solution.py:64
  1123.8 6.2 fusion.45
  1136.5 335.6 %fusion.88 = (f32[768,16]{0,1:T(8,128)S(1)}, f32[16,768]{1,0:T(8,128)S(1)}, f32[768,16]{0,1:T(8,128)S(1)}) fusion(f32[768,1536]{0,1:T(8,128)} %fusion.45, f32[1536,768]{1,0:T(8,128)} %fusion.87, f32[768,1664]{0,1:T(8,128)} %fusion.56), kind=kCustom, calls=%all-reduce-scatter.3 | all-reduce-scatter fusion | flops 4718593 | bytes 14696448
  1476.0 9.8 collective-permute-start.63
  1485.8 26.3 %collective-permute-start.30 = (f32[768,16]{0,1:T(8,128)S(1)}, f32[768,16]{0,1:T(8,128)S(1)}, u32[]{:S(2)}, u32[]{:S(2)}) collective-permute-start(f32[768,16]{0,1:T(8,128)S(1)} %get-tuple-element.14), channel_id=1, source_target_pairs={{0,31},{1,32},{2,33},{3,34},{4,35},{5,36},{6,37},{7,38},{8,39},{9,... | collective-permute-start | bytes 147464
  1527.7 7.0 collective-permute-start.21
  1700.8 68.8 %psum.15 = f32[]{:T(128)} all-reduce(f32[]{:T(128)S(6)} %add.151), channel_id=1, replica_groups=mesh['grp'=2,'dp'=64] {'grp','dp'}, use_global_device_ids=true, to_apply=%region_17.0 | all-reduce | flops 1 | bytes 8 | tf_op jit(solution)/shard_map/psum | solution.py:176
  1770.3 5.6 concatenate
  1790.8 6.5 collective-permute-start.69
  1798.0 24.2 %concatenate.1 = f32[524,768]{1,0:T(8,128)S(1)} concatenate(f32[12,768]{1,0:T(8,128)S(1)} %collective-permute-done.63, f32[16,768]{1,0:T(8,128)S(1)} %collective-permute-done.62, f32[16,768]{1,0:T(8,128)S(1)} %collective-permute-done.61, f32[16,768]{1,0:T(8,128)S(1)} %collective-permute-done.60, f32[16,768]{1,0:T(8,128)S(1)} %collective-permute-done.59, f32[16,768]{1,0:T(8,128)} %copy-done.9, ...), dimensions={0} | concatenate | bytes 3219456
  1831.0 5.3 collective-permute-start.65
  1846.3 6.8 concatenate.2
  (357 shorter events, 264.4 us)
Async XLA Ops:
  7.2 171.7 %all-reduce.13.cloned.1.call-start = ((), (), s32[]{:S(2)}) async-start(), calls=%async_computation.2 | async-start | bytes 524288 | tf_op jit(solution)/shard_map/psum | solution.py:110
  10.8 343.0 %all-gather.16.cloned.1.call-start = ((), (), s32[]{:S(2)}) async-start(), calls=%async_computation.4 | async-start | bytes 3170304 | tf_op jit(solution)/shard_map/all_gather | solution.py:83
  11.5 539.4 %all-gather.14.cloned.1.call-start = ((), (), s32[]{:S(2)}) async-start(), calls=%async_computation.3 | async-start | bytes 3170304 | tf_op jit(solution)/shard_map/all_gather | solution.py:79
  12.3 728.2 %all-gather.22.cloned.1.call-start = ((), (), s32[]{:S(2)}) async-start(), calls=%async_computation.7 | async-start | bytes 8519680 | tf_op jit(solution)/shard_map/all_gather | solution.py:60
  12.8 736.7 %all-gather.20.cloned.1.call-start = ((), (), s32[]{:S(2)}) async-start(), calls=%async_computation.6 | async-start | bytes 8519680 | tf_op jit(solution)/shard_map/all_gather | solution.py:54
  13.4 876.4 %all-reduce.15.cloned.1.call-start = ((), (), s32[]{:S(2)}) async-start(), calls=%async_computation.8 | async-start | bytes 524288
  735.7 350.2 %all-gather.18.cloned.1.call-start = ((), (), s32[]{:S(2)}) async-start(), calls=%async_computation.5 | async-start | bytes 3170304 | tf_op jit(solution)/shard_map/all_gather | solution.py:84
  736.4 381.1 %reduce-scatter.8.cloned.1.call-start = ((), (), s32[]{:S(2)}) async-start(), calls=%async_computation.1 | async-start | bytes 2555904 | tf_op jit(solution)/shard_map/reduce_scatter | solution.py:64
  773.3 926.2 %all-reduce.17.cloned.1.call-start = ((), (), s32[]{:S(2)}) async-start(), calls=%async_computation.9 | async-start | bytes 3145728
  1472.1 45.7 %collective-permute-start.87 = (f32[768,13]{0,1:T(8,128)S(1)}, f32[768,13]{0,1:T(8,128)S(1)}, u32[]{:S(2)}, u32[]{:S(2)}) collective-permute-start(f32[768,13]{0,1:T(8,128)S(1)} %slice.2), channel_id=1, source_target_pairs={{0,24},{1,25},{2,26},{3,27},{4,28},{5,29},{6,30},{7,31},{8,32},{9,... | collective-permute-start | bytes 119816
  1474.1 39.9 %collective-permute-start.31 = (f32[768,12]{0,1:T(8,128)S(1)}, f32[768,12]{0,1:T(8,128)S(1)}, u32[]{:S(2)}, u32[]{:S(2)}) collective-permute-start(f32[768,12]{0,1:T(8,128)S(1)} %slice), channel_id=1, source_target_pairs={{0,32},{1,33},{2,34},{3,35},{4,36},{5,37},{6,38},{7,39},{8,40},{9,... | collective-permute-start | bytes 110600
  1476.0 39.9 %collective-permute-start.63 = (f32[12,768]{1,0:T(8,128)S(1)}, f32[12,768]{1,0:T(8,128)S(1)}, u32[]{:S(2)}, u32[]{:S(2)}) collective-permute-start(f32[12,768]{1,0:T(8,128)S(1)} %slice.1), channel_id=1, source_target_pairs={{0,32},{1,33},{2,34},{3,35},{4,36},{5,37},{6,38},{7,39},{8,40},{9,... | collective-permute-start | bytes 110600
  1485.8 34.0 %collective-permute-start.30 = (f32[768,16]{0,1:T(8,128)S(1)}, f32[768,16]{0,1:T(8,128)S(1)}, u32[]{:S(2)}, u32[]{:S(2)}) collective-permute-start(f32[768,16]{0,1:T(8,128)S(1)} %get-tuple-element.14), channel_id=1, source_target_pairs={{0,31},{1,32},{2,33},{3,34},{4,35},{5,36},{6,37},{7,38},{8,39},{9,... | collective-permute-start | bytes 147464
  1687.5 88.5 %collective-permute-start.78 = (f32[768,16]{0,1:T(8,128)S(1)}, f32[768,16]{0,1:T(8,128)}, u32[]{:S(2)}, u32[]{:S(2)}) collective-permute-start(f32[768,16]{0,1:T(8,128)S(1)} %get-tuple-element.16), channel_id=1, source_target_pairs={{0,15},{1,16},{2,17},{3,18},{4,19},{5,20},{6,21},{7,22},{8,23},{9,... | collective-permute-start | bytes 147464
  1689.8 90.5 %collective-permute-start.77 = (f32[768,16]{0,1:T(8,128)S(1)}, f32[768,16]{0,1:T(8,128)}, u32[]{:S(2)}, u32[]{:S(2)}) collective-permute-start(f32[768,16]{0,1:T(8,128)S(1)} %get-tuple-element.16), channel_id=1, source_target_pairs={{0,14},{1,15},{2,16},{3,17},{4,18},{5,19},{6,20},{7,21},{8,22},{9,... | collective-permute-start | bytes 147464
  1692.6 91.3 %collective-permute-start.76 = (f32[768,16]{0,1:T(8,128)S(1)}, f32[768,16]{0,1:T(8,128)}, u32[]{:S(2)}, u32[]{:S(2)}) collective-permute-start(f32[768,16]{0,1:T(8,128)S(1)} %get-tuple-element.16), channel_id=1, source_target_pairs={{0,13},{1,14},{2,15},{3,16},{4,17},{5,18},{6,19},{7,20},{8,21},{9,... | collective-permute-start | bytes 147464
  1695.2 91.6 %collective-permute-start.75 = (f32[768,16]{0,1:T(8,128)S(1)}, f32[768,16]{0,1:T(8,128)}, u32[]{:S(2)}, u32[]{:S(2)}) collective-permute-start(f32[768,16]{0,1:T(8,128)S(1)} %get-tuple-element.16), channel_id=1, source_target_pairs={{0,12},{1,13},{2,14},{3,15},{4,16},{5,17},{6,18},{7,19},{8,20},{9,... | collective-permute-start | bytes 147464
  1697.5 93.4 %collective-permute-start.74 = (f32[768,16]{0,1:T(8,128)S(1)}, f32[768,16]{0,1:T(8,128)}, u32[]{:S(2)}, u32[]{:S(2)}) collective-permute-start(f32[768,16]{0,1:T(8,128)S(1)} %get-tuple-element.16), channel_id=1, source_target_pairs={{0,11},{1,12},{2,13},{3,14},{4,15},{5,16},{6,17},{7,18},{8,19},{9,... | collective-permute-start | bytes 147464
  1776.0 46.2 %collective-permute-start.73 = (f32[768,16]{0,1:T(8,128)S(1)}, f32[768,16]{0,1:T(8,128)S(1)}, u32[]{:S(2)}, u32[]{:S(2)}) collective-permute-start(f32[768,16]{0,1:T(8,128)S(1)} %get-tuple-element.16), channel_id=1, source_target_pairs={{0,10},{1,11},{2,12},{3,13},{4,14},{5,15},{6,16},{7,17},{8,18},{9,... | collective-permute-start | bytes 147464
  1780.3 43.9 %collective-permute-start.72 = (f32[768,16]{0,1:T(8,128)S(1)}, f32[768,16]{0,1:T(8,128)S(1)}, u32[]{:S(2)}, u32[]{:S(2)}) collective-permute-start(f32[768,16]{0,1:T(8,128)S(1)} %get-tuple-element.16), channel_id=1, source_target_pairs={{0,9},{1,10},{2,11},{3,12},{4,13},{5,14},{6,15},{7,16},{8,17},{9,1... | collective-permute-start | bytes 147464
  1783.9 44.3 %collective-permute-start.71 = (f32[768,16]{0,1:T(8,128)S(1)}, f32[768,16]{0,1:T(8,128)S(1)}, u32[]{:S(2)}, u32[]{:S(2)}) collective-permute-start(f32[768,16]{0,1:T(8,128)S(1)} %get-tuple-element.16), channel_id=1, source_target_pairs={{0,8},{1,9},{2,10},{3,11},{4,12},{5,13},{6,14},{7,15},{8,16},{9,17... | collective-permute-start | bytes 147464
  1786.8 44.1 %collective-permute-start.70 = (f32[768,16]{0,1:T(8,128)S(1)}, f32[768,16]{0,1:T(8,128)S(1)}, u32[]{:S(2)}, u32[]{:S(2)}) collective-permute-start(f32[768,16]{0,1:T(8,128)S(1)} %get-tuple-element.16), channel_id=1, source_target_pairs={{0,7},{1,8},{2,9},{3,10},{4,11},{5,12},{6,13},{7,14},{8,15},{9,16}... | collective-permute-start | bytes 147464
  1790.8 45.4 %collective-permute-start.69 = (f32[768,16]{0,1:T(8,128)S(1)}, f32[768,16]{0,1:T(8,128)S(1)}, u32[]{:S(2)}, u32[]{:S(2)}) collective-permute-start(f32[768,16]{0,1:T(8,128)S(1)} %get-tuple-element.16), channel_id=1, source_target_pairs={{0,6},{1,7},{2,8},{3,9},{4,10},{5,11},{6,12},{7,13},{8,14},{9,15},... | collective-permute-start | bytes 147464
  1822.2 16.6 collective-permute-start.68
  (128 other events, 3706.4 us)
Sparse Core Ops, SparseCore 0:
  12.7 144.8 all-reduce.12
  159.4 194.4 all-gather.15
  355.6 195.2 all-gather.13
  554.0 80.3 all-gather.21
  637.5 80.1 all-gather.19
  735.8 154.0 all-reduce.14
  891.6 194.2 all-gather.17
  1088.2 29.3 reduce-scatter.7
  1122.3 152.8 all-reduce.16
where the time goes:
time: 1870 us; the launch traced here: 1860 us
  blocking collectives  730 us (39%)
  waiting for transfers between devices  715 us (38%)
  starting transfers between devices  252 us (13%)
  local copies, waits for them, and re-layouts  80.9 us (4%)
  matrix products  41.4 us (2%)
  between operations  24.5 us (1%)
    unnamed x1, blocking collectives  336 us
    unnamed x90, starting transfers between devices  252 us
    all_gather x1, waiting for transfers between devices, local(): lax.all_gather(student_up, ('grp', 'dp'), axis=1, tiled=True)  192 us
    all_gather x1, waiting for transfers between devices, local(): lax.all_gather(student_head, ('grp', 'dp'), axis=1, tiled=True)  192 us
    all_gather x1, waiting for transfers between devices, local(): lax.all_gather(student_down, ('grp', 'dp'), axis=0, tiled=True)  173 us
    all_gather x1, blocking collectives, local(): lax.all_gather(student_proj, ('grp', 'dp'), axis=1, tiled=True)  164 us
    all_gather x1, blocking collectives, local(): gathered = lax.all_gather(image_emb, ('grp', 'dp'), axis=0, tiled=True)  161 us
    unnamed x99, waiting for transfers between devices  132 us
  transfers between devices with their start and end apart: 97, of which 15 were waited for; matrix products, arithmetic and copies ran while one was open for 25% of the time, Pallas kernels for 0%

commit v1 on v0

--- a/solution.py
+++ b/solution.py
@@ -1,3 +1,4 @@
+import functools
 import jax
 import jax.numpy as jnp
 from jax import lax
@@ -6,6 +7,15 @@
 CAP_LEN = 77
 PATCHES = 256
 IMG_DEV = 1
+
+
+def _bring_task(load, bus_axis):
+    base_arr = lax.all_to_all(jnp.stack(lax.axis_size(bus_axis) * [load]), bus_axis, 0, 0)
+    then = jnp.concatenate(base_arr, axis=1)
+    return then
+
+
+touch_notes = functools.partial(_bring_task, bus_axis=("grp", "dp"))
 
 
 def normalize_rows(values, gain):
@@ -81,7 +91,7 @@
     )
     down_whole, head_whole, proj_whole = (
         lax.all_gather(student_down, ("grp", "dp"), axis=0, tiled=True),
-        lax.all_gather(student_head, ("grp", "dp"), axis=1, tiled=True),
+        touch_notes(student_head),
         lax.all_gather(student_proj, ("grp", "dp"), axis=1, tiled=True),
     )
     student_act = gelu_tanh(gate_out).astype(jnp.bfloat16)

time: 1870 us -> 1710 us (0.914)
  waiting for transfers between devices: 715 us -> 494 us
  blocking collectives: 730 us -> 768 us
    all_gather x1 -> x0, waiting for transfers between devices: 192 us -> none  [local(): lax.all_gather(student_head, ('grp', 'dp'), axis=1, tiled=True)]
    all_gather x1, blocking collectives: 164 us -> 202 us  [local(): lax.all_gather(student_proj, ('grp', 'dp'), axis=1, tiled=True)]
    all_gather x1, waiting for transfers between devices: 173 us -> 144 us  [local(): lax.all_gather(student_down, ('grp', 'dp'), axis=0, tiled=True)]
    unnamed x127 -> x140, local copies, waits for them, and re-layouts: 75.7 us -> 73 us
    unnamed x99 -> x98, waiting for transfers between devices: 132 us -> 132 us
  transfers between devices with their start and end apart: 97 -> 97, of which waited for: 15 -> 14; matrix products, arithmetic and copies ran while one was open for 25% -> 28% of each run, Pallas kernels for 0% -> 0%
where the time goes in v1:
time: 1710 us; the launch traced here: 1700 us
  blocking collectives  768 us (45%)
  waiting for transfers between devices  494 us (29%)
  starting transfers between devices  262 us (15%)
  local copies, waits for them, and re-layouts  85 us (5%)
  matrix products  44 us (3%)
  between operations  25.1 us (1%)
  other arithmetic  18.9 us (1%)
    unnamed x1, blocking collectives  336 us
    unnamed x90, starting transfers between devices  251 us
    all_gather x1, blocking collectives, local(): lax.all_gather(student_proj, ('grp', 'dp'), axis=1, tiled=True)  202 us
    all_gather x1, waiting for transfers between devices, local(): lax.all_gather(student_up, ('grp', 'dp'), axis=1, tiled=True)  192 us
    all_gather x1, blocking collectives, local(): gathered = lax.all_gather(image_emb, ('grp', 'dp'), axis=0, tiled=True)  162 us
    all_gather x1, waiting for transfers between devices, local(): lax.all_gather(student_down, ('grp', 'dp'), axis=0, tiled=True)  144 us
    unnamed x98, waiting for transfers between devices  132 us
    unnamed x140, local copies, waits for them, and re-layouts  73 us
  transfers between devices with their start and end apart: 97, of which 14 were waited for; matrix products, arithmetic and copies ran while one was open for 28% of the time, Pallas kernels for 0%

profile of v1, /device:TPU:16, one launch (start us, length us, event | category | flops | bytes accessed | tf_op | source)
XLA Modules:
  0.0 1697.1 jit_solution(18348688529134525293)
XLA Ops:
  16.1 10.3 all-to-all-start
  26.5 201.6 %all-gather.5 = bf16[128,4,768]{2,1,0:T(4,128)(2,1)} all-gather(bf16[1,4,768]{2,1,0:T(4,128)(2,1)S(1)} %bitcast.97), channel_id=1, replica_groups=mesh['grp'=2,'dp'=64] {'grp','dp'}, dimensions={0}, use_global_device_ids=true | all-gather | bytes 792576 | tf_op jit(solution)/shard_map/all_gather | solution.py:95
  238.0 144.5 %all-gather.14.cloned.1.call-done = bf16[128,12,768]{2,1,0:T(8,128)(2,1)} async-done(((bf16[1,12,768]{2,1,0:T(8,128)(2,1)}), bf16[128,12,768]{2,1,0:T(8,128)(2,1)}) %all-gather.14.cloned.1.call-update) | async-done | bytes 2359312 | tf_op jit(solution)/shard_map/all_gather | solution.py:93
  382.5 4.9 reshape.204
  387.4 192.1 %all-gather.12.cloned.1.call-done = bf16[128,12,768]{2,1,0:T(8,128)(2,1)} async-done(((bf16[1,12,768]{2,1,0:T(8,128)(2,1)}), bf16[128,12,768]{2,1,0:T(8,128)(2,1)}) %all-gather.12.cloned.1.call-update) | async-done | bytes 2359312 | tf_op jit(solution)/shard_map/all_gather | solution.py:89
  579.5 4.9 reshape.202
  592.4 161.6 %all-gather.6 = f32[128,1,512]{2,1,0:T(1,128)S(1)} all-gather(f32[1,1,512]{2,1,0:T(1,128)S(1)} %bitcast.85), channel_id=2, replica_groups=mesh['grp'=2,'dp'=64] {'grp','dp'}, dimensions={0}, use_global_device_ids=true | all-gather | bytes 264192 | tf_op jit(solution)/shard_map/all_gather | solution.py:123
  769.3 9.1 reshape.208
  778.5 9.1 reshape.206
  787.6 14.7 convolution_convert_fusion
  807.0 114.9 %all-reduce.15.cloned.1.call-done = f32[128,512]{1,0:T(8,128)} async-done(((f32[128,512]{1,0:T(8,128)}), f32[128,512]{1,0:T(8,128)}) %all-reduce.15.cloned.1.call-update) | async-done | bytes 262160
  927.4 25.2 %reduce-scatter.8.cloned.1.call-done = bf16[256,1664]{1,0:T(8,128)(2,1)} async-done(((bf16[512,1664]{1,0:T(8,128)(2,1)}), bf16[256,1664]{1,0:T(8,128)(2,1)}) %reduce-scatter.8.cloned.1.call-update) | async-done | bytes 851984 | tf_op jit(solution)/shard_map/reduce_scatter | solution.py:74
  959.0 6.2 fusion.45
  971.7 335.7 %fusion.88 = (f32[768,16]{0,1:T(8,128)S(1)}, f32[16,768]{1,0:T(8,128)S(1)}, f32[768,16]{0,1:T(8,128)S(1)}) fusion(f32[768,1536]{0,1:T(8,128)} %fusion.45, f32[1536,768]{1,0:T(8,128)} %fusion.87, f32[768,1664]{0,1:T(8,128)} %fusion.56), kind=kCustom, calls=%all-reduce-scatter.3 | all-reduce-scatter fusion | flops 4718593 | bytes 14696448
  1311.3 9.6 collective-permute-start.63
  1320.9 26.3 %collective-permute-start.30 = (f32[768,16]{0,1:T(8,128)S(1)}, f32[768,16]{0,1:T(8,128)S(1)}, u32[]{:S(2)}, u32[]{:S(2)}) collective-permute-start(f32[768,16]{0,1:T(8,128)S(1)} %get-tuple-element.14), channel_id=1, source_target_pairs={{0,31},{1,32},{2,33},{3,34},{4,35},{5,36},{6,37},{7,38},{8,39},{9,... | collective-permute-start | bytes 147464
  1362.9 7.0 collective-permute-start.21
  1536.0 68.8 %psum.15 = f32[]{:T(128)} all-reduce(f32[]{:T(128)S(6)} %add.151), channel_id=1, replica_groups=mesh['grp'=2,'dp'=64] {'grp','dp'}, use_global_device_ids=true, to_apply=%region_17.0 | all-reduce | flops 1 | bytes 8 | tf_op jit(solution)/shard_map/psum | solution.py:186
  1605.5 5.6 concatenate
  1611.1 4.3 collective-permute-start.73
  1626.0 6.5 collective-permute-start.69
  1633.2 24.2 %concatenate.1 = f32[524,768]{1,0:T(8,128)S(1)} concatenate(f32[12,768]{1,0:T(8,128)S(1)} %collective-permute-done.63, f32[16,768]{1,0:T(8,128)S(1)} %collective-permute-done.62, f32[16,768]{1,0:T(8,128)S(1)} %collective-permute-done.61, f32[16,768]{1,0:T(8,128)S(1)} %collective-permute-done.60, f32[16,768]{1,0:T(8,128)S(1)} %collective-permute-done.59, f32[16,768]{1,0:T(8,128)} %copy-done.14, ...), dimensions={0} | concatenate | bytes 3219456
  1666.1 5.3 collective-permute-start.65
  1681.4 6.8 concatenate.2
  (371 shorter events, 272.8 us)
Async XLA Ops:
  7.2 228.7 %all-reduce.13.cloned.1.call-start = ((), (), s32[]{:S(2)}) async-start(), calls=%async_computation.3 | async-start | bytes 524288 | tf_op jit(solution)/shard_map/psum | solution.py:120
  10.8 371.8 %all-gather.14.cloned.1.call-start = ((), (), s32[]{:S(2)}) async-start(), calls=%async_computation.5 | async-start | bytes 3170304 | tf_op jit(solution)/shard_map/all_gather | solution.py:93
  11.5 568.0 %all-gather.12.cloned.1.call-start = ((), (), s32[]{:S(2)}) async-start(), calls=%async_computation.4 | async-start | bytes 3170304 | tf_op jit(solution)/shard_map/all_gather | solution.py:89
  12.3 757.1 %all-gather.18.cloned.1.call-start = ((), (), s32[]{:S(2)}) async-start(), calls=%async_computation.7 | async-start | bytes 8519680 | tf_op jit(solution)/shard_map/all_gather | solution.py:70
  12.8 765.6 %all-gather.16.cloned.1.call-start = ((), (), s32[]{:S(2)}) async-start(), calls=%async_computation.6 | async-start | bytes 8519680 | tf_op jit(solution)/shard_map/all_gather | solution.py:64
  16.1 786.4 %all-to-all-start = ((bf16[128,768,13]{1,2,0:T(8,128)(2,1)}), bf16[128,768,13]{1,2,0:T(8,128)(2,1)S(1)}, u32[]{:S(2)}, u32[]{:S(2)}) async-start(bf16[128,768,13]{1,2,0:T(8,128)(2,1)} %stack.2), calls=%async_computation | async-start | bytes 6291456 | tf_op jit(solution)/shard_map/all_to_all | solution.py:13
  26.4 895.4 %all-reduce.15.cloned.1.call-start = ((), (), s32[]{:S(2)}) async-start(), calls=%async_computation.8 | async-start | bytes 524288
  768.8 183.8 %reduce-scatter.8.cloned.1.call-start = ((), (), s32[]{:S(2)}) async-start(), calls=%async_computation.2 | async-start | bytes 2555904 | tf_op jit(solution)/shard_map/reduce_scatter | solution.py:74
  802.3 732.4 %all-reduce.17.cloned.1.call-start = ((), (), s32[]{:S(2)}) async-start(), calls=%async_computation.9 | async-start | bytes 3145728
  1307.4 45.6 %collective-permute-start.87 = (f32[768,13]{0,1:T(8,128)S(1)}, f32[768,13]{0,1:T(8,128)S(1)}, u32[]{:S(2)}, u32[]{:S(2)}) collective-permute-start(f32[768,13]{0,1:T(8,128)S(1)} %slice.2), channel_id=1, source_target_pairs={{0,24},{1,25},{2,26},{3,27},{4,28},{5,29},{6,30},{7,31},{8,32},{9,... | collective-permute-start | bytes 119816
  1309.4 39.8 %collective-permute-start.31 = (f32[768,12]{0,1:T(8,128)S(1)}, f32[768,12]{0,1:T(8,128)S(1)}, u32[]{:S(2)}, u32[]{:S(2)}) collective-permute-start(f32[768,12]{0,1:T(8,128)S(1)} %slice), channel_id=1, source_target_pairs={{0,32},{1,33},{2,34},{3,35},{4,36},{5,37},{6,38},{7,39},{8,40},{9,... | collective-permute-start | bytes 110600
  1311.3 39.8 %collective-permute-start.63 = (f32[12,768]{1,0:T(8,128)S(1)}, f32[12,768]{1,0:T(8,128)S(1)}, u32[]{:S(2)}, u32[]{:S(2)}) collective-permute-start(f32[12,768]{1,0:T(8,128)S(1)} %slice.1), channel_id=1, source_target_pairs={{0,32},{1,33},{2,34},{3,35},{4,36},{5,37},{6,38},{7,39},{8,40},{9,... | collective-permute-start | bytes 110600
  1320.9 34.0 %collective-permute-start.30 = (f32[768,16]{0,1:T(8,128)S(1)}, f32[768,16]{0,1:T(8,128)S(1)}, u32[]{:S(2)}, u32[]{:S(2)}) collective-permute-start(f32[768,16]{0,1:T(8,128)S(1)} %get-tuple-element.14), channel_id=1, source_target_pairs={{0,31},{1,32},{2,33},{3,34},{4,35},{5,36},{6,37},{7,38},{8,39},{9,... | collective-permute-start | bytes 147464
  1522.7 88.5 %collective-permute-start.78 = (f32[768,16]{0,1:T(8,128)S(1)}, f32[768,16]{0,1:T(8,128)}, u32[]{:S(2)}, u32[]{:S(2)}) collective-permute-start(f32[768,16]{0,1:T(8,128)S(1)} %get-tuple-element.16), channel_id=1, source_target_pairs={{0,15},{1,16},{2,17},{3,18},{4,19},{5,20},{6,21},{7,22},{8,23},{9,... | collective-permute-start | bytes 147464
  1525.2 90.3 %collective-permute-start.77 = (f32[768,16]{0,1:T(8,128)S(1)}, f32[768,16]{0,1:T(8,128)}, u32[]{:S(2)}, u32[]{:S(2)}) collective-permute-start(f32[768,16]{0,1:T(8,128)S(1)} %get-tuple-element.16), channel_id=1, source_target_pairs={{0,14},{1,15},{2,16},{3,17},{4,18},{5,19},{6,20},{7,21},{8,22},{9,... | collective-permute-start | bytes 147464
  1527.8 91.3 %collective-permute-start.76 = (f32[768,16]{0,1:T(8,128)S(1)}, f32[768,16]{0,1:T(8,128)}, u32[]{:S(2)}, u32[]{:S(2)}) collective-permute-start(f32[768,16]{0,1:T(8,128)S(1)} %get-tuple-element.16), channel_id=1, source_target_pairs={{0,13},{1,14},{2,15},{3,16},{4,17},{5,18},{6,19},{7,20},{8,21},{9,... | collective-permute-start | bytes 147464
  1530.3 91.7 %collective-permute-start.75 = (f32[768,16]{0,1:T(8,128)S(1)}, f32[768,16]{0,1:T(8,128)}, u32[]{:S(2)}, u32[]{:S(2)}) collective-permute-start(f32[768,16]{0,1:T(8,128)S(1)} %get-tuple-element.16), channel_id=1, source_target_pairs={{0,12},{1,13},{2,14},{3,15},{4,16},{5,17},{6,18},{7,19},{8,20},{9,... | collective-permute-start | bytes 147464
  1532.6 93.4 %collective-permute-start.74 = (f32[768,16]{0,1:T(8,128)S(1)}, f32[768,16]{0,1:T(8,128)}, u32[]{:S(2)}, u32[]{:S(2)}) collective-permute-start(f32[768,16]{0,1:T(8,128)S(1)} %get-tuple-element.16), channel_id=1, source_target_pairs={{0,11},{1,12},{2,13},{3,14},{4,15},{5,16},{6,17},{7,18},{8,19},{9,... | collective-permute-start | bytes 147464
  1611.1 46.2 %collective-permute-start.73 = (f32[768,16]{0,1:T(8,128)S(1)}, f32[768,16]{0,1:T(8,128)S(1)}, u32[]{:S(2)}, u32[]{:S(2)}) collective-permute-start(f32[768,16]{0,1:T(8,128)S(1)} %get-tuple-element.16), channel_id=1, source_target_pairs={{0,10},{1,11},{2,12},{3,13},{4,14},{5,15},{6,16},{7,17},{8,18},{9,... | collective-permute-start | bytes 147464
  1615.5 43.9 %collective-permute-start.72 = (f32[768,16]{0,1:T(8,128)S(1)}, f32[768,16]{0,1:T(8,128)S(1)}, u32[]{:S(2)}, u32[]{:S(2)}) collective-permute-start(f32[768,16]{0,1:T(8,128)S(1)} %get-tuple-element.16), channel_id=1, source_target_pairs={{0,9},{1,10},{2,11},{3,12},{4,13},{5,14},{6,15},{7,16},{8,17},{9,1... | collective-permute-start | bytes 147464
  1619.0 44.3 %collective-permute-start.71 = (f32[768,16]{0,1:T(8,128)S(1)}, f32[768,16]{0,1:T(8,128)S(1)}, u32[]{:S(2)}, u32[]{:S(2)}) collective-permute-start(f32[768,16]{0,1:T(8,128)S(1)} %get-tuple-element.16), channel_id=1, source_target_pairs={{0,8},{1,9},{2,10},{3,11},{4,12},{5,13},{6,14},{7,15},{8,16},{9,17... | collective-permute-start | bytes 147464
  1622.0 44.1 %collective-permute-start.70 = (f32[768,16]{0,1:T(8,128)S(1)}, f32[768,16]{0,1:T(8,128)S(1)}, u32[]{:S(2)}, u32[]{:S(2)}) collective-permute-start(f32[768,16]{0,1:T(8,128)S(1)} %get-tuple-element.16), channel_id=1, source_target_pairs={{0,7},{1,8},{2,9},{3,10},{4,11},{5,12},{6,13},{7,14},{8,15},{9,16}... | collective-permute-start | bytes 147464
  1626.0 45.4 %collective-permute-start.69 = (f32[768,16]{0,1:T(8,128)S(1)}, f32[768,16]{0,1:T(8,128)S(1)}, u32[]{:S(2)}, u32[]{:S(2)}) collective-permute-start(f32[768,16]{0,1:T(8,128)S(1)} %get-tuple-element.16), channel_id=1, source_target_pairs={{0,6},{1,7},{2,8},{3,9},{4,10},{5,11},{6,12},{7,13},{8,14},{9,15},... | collective-permute-start | bytes 147464
  1657.4 16.6 collective-permute-start.68
  (135 other events, 3828.2 us)
Sparse Core Ops, SparseCore 0:
  12.7 173.7 all-reduce.12
  188.2 194.2 all-gather.13
  384.2 195.2 all-gather.11
  582.6 80.4 all-gather.17
  666.2 80.2 all-gather.15
  768.9 152.8 all-reduce.14
  924.2 28.3 reduce-scatter.7
  957.3 153.6 all-reduce.16
